TPU v7x, 32 devices: a whole 2x2x4 slice. The times are simulated.
32 devices in a mesh: qrow: 4 (over y, x), kcol: 8 (over z, core).
Axes of the slice: x: 2, y: 2, z: 4, core: 2. Of those that a mesh axis runs over, the one named last changes fastest.
Arguments:
- queries: bfloat16 [8192, 512], P(('qrow', 'kcol')), may hold values from -6 to 6
- keys: bfloat16 [8192, 128], P(('kcol', 'qrow')), may hold values from -6 to 6
- values: bfloat16 [8192, 128], P(('kcol', 'qrow')), may hold values from -6 to 6
- block_mask: int32 [64, 64], replicated, may hold values from 0 to 1, as said below
Outputs:
- attended: float32 [8192, 512], P(('qrow', 'kcol'))
Inputs may be any that keep to these rules, and one draw needn't show every extreme that they name: block_mask[a, b] is 1 only where b <= a, and always where 0 <= a - b < 3.
All inputs are finite; a program needn't handle non-finite values.
Results may differ from a plain program's by a relative error of at most 0.0022.
Values may be sent and summed in bfloat16 or wider, within the bound.
A program may use at most 64 MiB of HBM per device.

v0:
```python
import math

import jax
import jax.numpy as jnp
from jax import lax
from jax.sharding import PartitionSpec as P

H = 4
DH = 128
BLOCK = 128


NEG_FILL = -1e30


def shards(queries, keys, values, block_mask):
    inv_root = 1.0 / math.sqrt(DH)
    tok_count = queries.shape[0]
    col_count = lax.axis_size("kcol")
    query_tile = tok_count * col_count
    key_tile, value_tile = (
        lax.all_gather(keys, "qrow", axis=0, tiled=True),
        lax.all_gather(values, "qrow", axis=0, tiled=True),
    )
    key_width = key_tile.shape[0]
    block_count = key_width // BLOCK
    value_blocks = value_tile.reshape(block_count, BLOCK, DH)
    query_first = lax.axis_index("qrow") * query_tile
    key_first = lax.axis_index("kcol") * key_width
    tile_mask = lax.dynamic_slice(
        block_mask, (query_first // BLOCK, key_first // BLOCK), (query_tile // BLOCK, block_count)
    )
    column_mask = jnp.repeat(tile_mask, BLOCK, 1)
    key_pos = key_first + jnp.arange(key_width, dtype=jnp.int32)
    query_piece = lax.all_gather(queries, "kcol", axis=0, tiled=True)
    row_count = query_piece.shape[0]
    part_rows = math.gcd(row_count, 512)
    part_count = row_count // part_rows
    stacked = query_piece.reshape(part_count, part_rows, H, DH)

    def one_part(index):
        start = index * part_rows
        query_heads = lax.dynamic_index_in_dim(stacked, index, 0, keepdims=False)
        scores = (
            jnp.einsum("rhd,kd->hrk", query_heads, key_tile, preferred_element_type=jnp.float32)
            * inv_root
        )
        local_rows = start + jnp.arange(part_rows, dtype=jnp.int32)
        listed = jnp.take(column_mask, local_rows // BLOCK, axis=0) == 1
        permitted = listed & (key_pos[None, :] <= (query_first + local_rows)[:, None])
        permitted = permitted.reshape(part_rows, block_count, BLOCK)
        scores = scores.reshape(H, part_rows, block_count, BLOCK)
        scores = jnp.where(permitted[None], scores, NEG_FILL)
        block_top = jnp.max(scores, axis=3)
        weights = jnp.where(permitted[None], jnp.exp(scores - block_top[..., None]), 0.0).astype(
            jnp.bfloat16
        )
        block_mass = jnp.sum(weights.astype(jnp.float32), axis=3)
        block_out = jnp.einsum(
            "hrkb,kbd->hrkd", weights, value_blocks, preferred_element_type=jnp.float32
        )
        row_top = jnp.max(block_top, axis=2)
        factor = jnp.exp(block_top - row_top[..., None])
        mixed = jnp.sum(block_out * factor[..., None], axis=2)
        row_mass = jnp.sum(block_mass * factor, axis=2)
        mixed = jnp.transpose(mixed, (1, 0, 2))
        return (mixed.reshape(part_rows, H * DH), row_top.T, row_mass.T)

    mixed_all, top_all, mass_all = lax.map(one_part, jnp.arange(part_count, dtype=jnp.int32))
    outputs = mixed_all.reshape(row_count, H * DH)
    highest = top_all.reshape(row_count, H)
    masses = mass_all.reshape(row_count, H)
    outputs, highest, masses = (outputs, highest, masses)
    overall = lax.pmax(highest.astype(jnp.bfloat16), "kcol").astype(highest.dtype)
    factor = jnp.exp(highest - overall)
    scaled_out = (outputs.reshape(query_tile, H, DH) * factor[..., None]).reshape(
        query_tile, H * DH
    )
    scaled_mass = masses * factor
    total_mass = lax.psum(scaled_mass, "kcol")
    numerator = lax.psum_scatter(scaled_out, "kcol", scatter_dimension=0, tiled=True)
    own_mass = lax.dynamic_slice_in_dim(
        total_mass, lax.axis_index("kcol") * tok_count, tok_count, 0
    )
    result = numerator.reshape(tok_count, H, DH) / own_mass[..., None]
    return result.reshape(tok_count, H * DH)


def solution(mesh):
    placed = (P(("qrow", "kcol"), None), P(("kcol", "qrow"), None), P(("kcol", "qrow"), None), P())
    return jax.shard_map(
        shards, mesh=mesh, in_specs=placed, out_specs=P(("qrow", "kcol"), None), check_vma=False
    )
```

profile of v0, /device:TPU:0, one launch (start us, length us, event | category | flops | bytes accessed | tf_op | source)
XLA Modules:
  0.0 247.2 jit_solution(12887789881885256544)
XLA Ops:
  8.2 10.7 %all_gather.10 = bf16[1024,128]{1,0:T(8,128)(2,1)S(1)} all-gather(bf16[256,128]{1,0:T(8,128)(2,1)} %param.7), channel_id=1, replica_groups=mesh['qrow'=4,'kcol'=8] {'qrow'}, dimensions={0}, use_global_device_ids=true | all-gather | bytes 327680 | tf_op jit(solution)/shard_map/all_gather | solution.py:22
  18.9 8.7 %all_gather.11 = bf16[1024,128]{1,0:T(8,128)(2,1)S(1)} all-gather(bf16[256,128]{1,0:T(8,128)(2,1)} %param.8), channel_id=1, replica_groups=mesh['qrow'=4,'kcol'=8] {'qrow'}, dimensions={0}, use_global_device_ids=true | all-gather | bytes 327680 | tf_op jit(solution)/shard_map/all_gather | solution.py:23
  27.6 13.3 %all-gather.2.cloned.1.call-done = bf16[2048,512]{1,0:T(8,128)(2,1)} async-done(((bf16[256,512]{1,0:T(8,128)(2,1)}), bf16[2048,512]{1,0:T(8,128)(2,1)}) %all-gather.2.cloned.1.call-update) | async-done | bytes 2097168 | tf_op jit(solution)/shard_map/all_gather | solution.py:35
  40.8 4.0 %reshape.149 = bf16[4,512,4,128]{3,2,1,0:T(4,128)(2,1)} reshape(bf16[2048,512]{1,0:T(8,128)(2,1)} %all-gather.2.cloned.1.call-done) | data formatting | bytes 4194304 | tf_op jit(solution)/shard_map/reshape | solution.py:39
  44.8 106.9 %while.17 = (s32[]{:T(128)}, f32[4,512,512]{2,1,0:T(8,128)}, f32[4,512,4]{1,2,0:T(4,128)S(1)}, f32[4,512,4]{1,2,0:T(4,128)S(1)}, s32[4]{0:T(128)S(1)}, /*index=5...) while((s32[]{:T(128)}, f32[4,512,512]{2,1,0:T(8,128)}, ...), condition=%wide.region_6.7_spmd.clone, body=%wide.region_0.6_spmd.clone.sunk | while | flops 1119654400 | bytes 60582128 | solution.py:69
  52.1 2.6 %fusion.30 = pred[512,8,128]{2,1,0:T(8,128)(4,1)S(1)} fusion(s32[64,8,8,128]{3,2,1,0:T(8,128)S(1)} %copy.63, s32[8,128]{1,0:T(8,128)S(1)} %fusion.28, s32[512]{0:T(512)S(1)} %fusion.29, pred[512]{0:T(512)(128)(4,1)S(1)} %compare_and_fusion.2), kind=kLoop, calls=%fused_computation.16.clone.1 | loop fusion | flops 2097152 | bytes 2628096 | tf_op jit(solution)/shard_map/while/body/eval_jaxpr/and | solution.py:50
  56.8 2.3 fusion.33
  59.1 5.3 %convert_reduce_fusion.2 = f32[4,512,8]{1,0,2:T(4,128)S(1)} fusion(f32[4,512,8]{1,0,2:T(4,128)S(1)} %fusion.33, pred[512,8,128]{2,0,1:T(8,128)(4,1)S(1)} %copy.64, f32[512,4,1024]{2,0,1:T(8,128)S(1)} %get-tuple-element.311), kind=kLoop, calls=%fused_computation.8.clone.1 | loop fusion | flops 14663680 | bytes 9043968 | tf_op jit(solution)/shard_map/while/body/eval_jaxpr/reduce_sum | solution.py:58
  64.5 5.3 %fusion.34 = f32[4,512,128]{2,1,0:T(8,128)S(1)} fusion(f32[4,512,8]{1,0,2:T(4,128)S(1)} %get-tuple-element.313, bf16[8,128,128]{2,1,0:T(8,128)(2,1)S(1)} %get-tuple-element.355, f32[4,512,8]{1,0,2:T(4,128)S(1)} %fusion.33, pred[512,8,128]{2,0,1:T(8,128)(4,1)S(1)} %copy.64, f32[512,4,1024]{2,0,1:T(8,128)S(1)} %get-tuple-element.311), kind=kOutput, calls=%fused_computation.5.clone.1 | convolution fusion | flops 551288832 | bytes 10354688 | tf_op jit(solution)/shard_map/while/body/eval_jaxpr/hrkb,kbd->hrkd/dot_general | solution.py:59
  78.8 2.6 %fusion.30 = pred[512,8,128]{2,1,0:T(8,128)(4,1)S(1)} fusion(s32[64,8,8,128]{3,2,1,0:T(8,128)S(1)} %copy.63, s32[8,128]{1,0:T(8,128)S(1)} %fusion.28, s32[512]{0:T(512)S(1)} %fusion.29, pred[512]{0:T(512)(128)(4,1)S(1)} %compare_and_fusion.2), kind=kLoop, calls=%fused_computation.16.clone.1 | loop fusion | flops 2097152 | bytes 2628096 | tf_op jit(solution)/shard_map/while/body/eval_jaxpr/and | solution.py:50
  85.8 5.3 %convert_reduce_fusion.2 = f32[4,512,8]{1,0,2:T(4,128)S(1)} fusion(f32[4,512,8]{1,0,2:T(4,128)S(1)} %fusion.33, pred[512,8,128]{2,0,1:T(8,128)(4,1)S(1)} %copy.64, f32[512,4,1024]{2,0,1:T(8,128)S(1)} %get-tuple-element.311), kind=kLoop, calls=%fused_computation.8.clone.1 | loop fusion | flops 14663680 | bytes 9043968 | tf_op jit(solution)/shard_map/while/body/eval_jaxpr/reduce_sum | solution.py:58
  91.2 5.3 %fusion.34 = f32[4,512,128]{2,1,0:T(8,128)S(1)} fusion(f32[4,512,8]{1,0,2:T(4,128)S(1)} %get-tuple-element.313, bf16[8,128,128]{2,1,0:T(8,128)(2,1)S(1)} %get-tuple-element.355, f32[4,512,8]{1,0,2:T(4,128)S(1)} %fusion.33, pred[512,8,128]{2,0,1:T(8,128)(4,1)S(1)} %copy.64, f32[512,4,1024]{2,0,1:T(8,128)S(1)} %get-tuple-element.311), kind=kOutput, calls=%fused_computation.5.clone.1 | convolution fusion | flops 551288832 | bytes 10354688 | tf_op jit(solution)/shard_map/while/body/eval_jaxpr/hrkb,kbd->hrkd/dot_general | solution.py:59
  105.6 2.6 %fusion.30 = pred[512,8,128]{2,1,0:T(8,128)(4,1)S(1)} fusion(s32[64,8,8,128]{3,2,1,0:T(8,128)S(1)} %copy.63, s32[8,128]{1,0:T(8,128)S(1)} %fusion.28, s32[512]{0:T(512)S(1)} %fusion.29, pred[512]{0:T(512)(128)(4,1)S(1)} %compare_and_fusion.2), kind=kLoop, calls=%fused_computation.16.clone.1 | loop fusion | flops 2097152 | bytes 2628096 | tf_op jit(solution)/shard_map/while/body/eval_jaxpr/and | solution.py:50
  110.3 2.3 fusion.33
  112.6 5.3 %convert_reduce_fusion.2 = f32[4,512,8]{1,0,2:T(4,128)S(1)} fusion(f32[4,512,8]{1,0,2:T(4,128)S(1)} %fusion.33, pred[512,8,128]{2,0,1:T(8,128)(4,1)S(1)} %copy.64, f32[512,4,1024]{2,0,1:T(8,128)S(1)} %get-tuple-element.311), kind=kLoop, calls=%fused_computation.8.clone.1 | loop fusion | flops 14663680 | bytes 9043968 | tf_op jit(solution)/shard_map/while/body/eval_jaxpr/reduce_sum | solution.py:58
  118.0 5.3 %fusion.34 = f32[4,512,128]{2,1,0:T(8,128)S(1)} fusion(f32[4,512,8]{1,0,2:T(4,128)S(1)} %get-tuple-element.313, bf16[8,128,128]{2,1,0:T(8,128)(2,1)S(1)} %get-tuple-element.355, f32[4,512,8]{1,0,2:T(4,128)S(1)} %fusion.33, pred[512,8,128]{2,0,1:T(8,128)(4,1)S(1)} %copy.64, f32[512,4,1024]{2,0,1:T(8,128)S(1)} %get-tuple-element.311), kind=kOutput, calls=%fused_computation.5.clone.1 | convolution fusion | flops 551288832 | bytes 10354688 | tf_op jit(solution)/shard_map/while/body/eval_jaxpr/hrkb,kbd->hrkd/dot_general | solution.py:59
  132.3 2.6 %fusion.30 = pred[512,8,128]{2,1,0:T(8,128)(4,1)S(1)} fusion(s32[64,8,8,128]{3,2,1,0:T(8,128)S(1)} %copy.63, s32[8,128]{1,0:T(8,128)S(1)} %fusion.28, s32[512]{0:T(512)S(1)} %fusion.29, pred[512]{0:T(512)(128)(4,1)S(1)} %compare_and_fusion.2), kind=kLoop, calls=%fused_computation.16.clone.1 | loop fusion | flops 2097152 | bytes 2628096 | tf_op jit(solution)/shard_map/while/body/eval_jaxpr/and | solution.py:50
  139.3 5.3 %convert_reduce_fusion.2 = f32[4,512,8]{1,0,2:T(4,128)S(1)} fusion(f32[4,512,8]{1,0,2:T(4,128)S(1)} %fusion.33, pred[512,8,128]{2,0,1:T(8,128)(4,1)S(1)} %copy.64, f32[512,4,1024]{2,0,1:T(8,128)S(1)} %get-tuple-element.311), kind=kLoop, calls=%fused_computation.8.clone.1 | loop fusion | flops 14663680 | bytes 9043968 | tf_op jit(solution)/shard_map/while/body/eval_jaxpr/reduce_sum | solution.py:58
  144.7 5.3 %fusion.34 = f32[4,512,128]{2,1,0:T(8,128)S(1)} fusion(f32[4,512,8]{1,0,2:T(4,128)S(1)} %get-tuple-element.313, bf16[8,128,128]{2,1,0:T(8,128)(2,1)S(1)} %get-tuple-element.355, f32[4,512,8]{1,0,2:T(4,128)S(1)} %fusion.33, pred[512,8,128]{2,0,1:T(8,128)(4,1)S(1)} %copy.64, f32[512,4,1024]{2,0,1:T(8,128)S(1)} %get-tuple-element.311), kind=kOutput, calls=%fused_computation.5.clone.1 | convolution fusion | flops 551288832 | bytes 10354688 | tf_op jit(solution)/shard_map/while/body/eval_jaxpr/hrkb,kbd->hrkd/dot_general | solution.py:59
  151.7 27.4 %pmax.7 = bf16[2048,4]{0,1:T(4,128)(2,1)S(1)} all-reduce(bf16[2048,4]{0,1:T(4,128)(2,1)S(1)} %convert_element_type.18), channel_id=1, replica_groups=mesh['qrow'=4,'kcol'=8] {'kcol'}, use_global_device_ids=true, to_apply=%region_7.8 | all-reduce | flops 8192 | bytes 32768 | tf_op jit(solution)/shard_map/pmax | solution.py:74
  179.6 4.7 %mul.61 = f32[2048,4,128]{2,1,0:T(4,128)S(1)} broadcast(f32[2048,4]{1,0:T(8,128)S(1)} %copy.22), dimensions={0,1} | broadcast | bytes 4227072 | tf_op jit(solution)/shard_map/mul | solution.py:76
  184.3 5.2 %bitcast_multiply_fusion.1 = f32[2048,512]{1,0:T(8,128)} fusion(f32[256,8,4,128]{3,2,1,0:T(4,128)S(1)} %bitcast.120, f32[4,512,512]{2,1,0:T(8,128)} %get-tuple-element.145), kind=kLoop, calls=%fused_computation.48 | loop fusion | flops 1048576 | bytes 12582912 | tf_op jit(solution)/shard_map/mul | solution.py:76
  189.5 27.4 %psum.7 = f32[2048,4]{0,1:T(4,128)S(1)} all-reduce(f32[2048,4]{0,1:T(4,128)S(1)} %get-tuple-element.232), channel_id=1, replica_groups=mesh['qrow'=4,'kcol'=8] {'kcol'}, use_global_device_ids=true, to_apply=%region_9.10 | all-reduce | flops 8192 | bytes 65536 | tf_op jit(solution)/shard_map/psum | solution.py:80
  217.0 21.1 %reduce-scatter.2.cloned.1.call-done = f32[256,512]{1,0:T(8,128)} async-done(((f32[2048,512]{1,0:T(8,128)}), f32[256,512]{1,0:T(8,128)}) %reduce-scatter.2.cloned.1.call-update) | async-done | bytes 524304 | tf_op jit(solution)/shard_map/reduce_scatter | solution.py:81
  (98 shorter events, 44.3 us)
Async XLA Ops:
  6.5 34.3 %all-gather.2.cloned.1.call-start = ((), (), s32[]{:S(2)}) async-start(), calls=%async_computation.1 | async-start | bytes 2359296 | tf_op jit(solution)/shard_map/all_gather | solution.py:35
  7.3 230.9 %reduce-scatter.2.cloned.1.call-start = ((), (), s32[]{:S(2)}) async-start(), calls=%async_computation.2 | async-start | bytes 4718592 | tf_op jit(solution)/shard_map/reduce_scatter | solution.py:81
Sparse Core Ops, SparseCore 0:
  8.9 31.8 all-gather.1
  189.6 48.4 reduce-scatter.1
where the time goes:
time: 248 us; the launch traced here: 247 us
  blocking collectives  74.2 us (30%)
  other arithmetic  50.4 us (20%)
  local copies, waits for them, and re-layouts  35.4 us (14%)
  waiting for transfers between devices  35.1 us (14%)
  matrix products  28.7 us (12%)
  between operations  13.5 us (5%)
  loops' own time  9.72 us (4%)
    pmax x1, blocking collectives, shards(): lax.pmax(highest.astype(jnp.bfloat16), 'kcol').astype(highest.dtype)  27.4 us
    psum x1, blocking collectives, shards(): total_mass = lax.psum(scaled_mass, 'kcol')  27.4 us
    reduce_sum x4, other arithmetic, one_part(): block_mass = jnp.sum(weights.astype(jnp.float32), axis=3)  21.3 us
    dot_general x4, matrix products, one_part(): jnp.einsum('hrkb,kbd->hrkd', weights, value_blocks, preferred_element_typ...  21.2 us
    reduce_scatter x1, waiting for transfers between devices, shards(): lax.psum_scatter(scaled_out, 'kcol', scatter_dimension=0, tiled=True)  21.1 us
    all_gather x1, waiting for transfers between devices, shards(): query_piece = lax.all_gather(queries, 'kcol', axis=0, tiled=True)  13.3 us
    and x8, other arithmetic, one_part(): listed & (key_pos[None, :] <= (query_first + local_rows)[:, None])  12.5 us
    all_gather x1, blocking collectives, shards(): lax.all_gather(keys, 'qrow', axis=0, tiled=True)  10.7 us
  transfers between devices with their start and end apart: 2, of which 2 were waited for; matrix products, arithmetic and copies ran while one was open for 0% of the time, Pallas kernels for 0%

commit v1 on v0

v1 whole, which is shorter than its diff:
```python
import math

import jax
import jax.numpy as jnp
from jax import lax
from jax.experimental import pallas as pl
from jax.experimental.pallas import tpu as pltpu
from jax.sharding import PartitionSpec as P

H = 4
DH = 128
BLOCK = 128
GROUP = 4
NEG_FILL = -1e30
SCALE = math.log2(math.e) / math.sqrt(DH)


def over_keys(values, weights):
    return lax.dot_general(
        values, weights, (((0,), (0,)), ((), ())), preferred_element_type=jnp.float32
    )


def attend(mask_ref, q_ref, k_ref, v_ref, out_ref, listed, total):
    own_blocks = q_ref.shape[0] // BLOCK
    device = lax.axis_index("qrow") * lax.axis_size("kcol") + lax.axis_index("kcol")

    def rows_of(ref, block):
        return ref[pl.ds(pl.multiple_of(block * BLOCK, BLOCK), BLOCK), :]

    for own in range(own_blocks):
        rows = pl.ds(own * BLOCK, BLOCK)
        row = device * own_blocks + own
        flipped = jnp.concatenate(
            [q_ref[rows, h * DH : (h + 1) * DH].T for h in range(H)], axis=1
        )

        def note(j, count):
            listed[count] = j
            return count + mask_ref[row, j]

        count = lax.fori_loop(0, row, note, jnp.int32(0))

        def scores_of(block):
            return jnp.dot(rows_of(k_ref, block), flipped, preferred_element_type=jnp.float32)

        scores = scores_of(row)
        key_at = lax.broadcasted_iota(jnp.int32, scores.shape, 0)
        query_at = lax.broadcasted_iota(jnp.int32, scores.shape, 1) % BLOCK
        scores = jnp.where(key_at <= query_at, scores, NEG_FILL)
        top = jnp.max(scores, axis=0, keepdims=True)
        weights = jnp.exp2(scores * SCALE - top * SCALE)
        mass = jnp.sum(weights, axis=0, keepdims=True)
        total[...] = over_keys(rows_of(v_ref, row), weights.astype(jnp.bfloat16))

        def add(start, size, state):
            top, mass = state
            blocks = [listed[start + g] for g in range(size)]
            scores = [scores_of(b) for b in blocks]
            high = scores[0]
            for s in scores[1:]:
                high = jnp.maximum(high, s)
            new_top = jnp.maximum(top, jnp.max(high, axis=0, keepdims=True))
            fade = jnp.exp2((top - new_top) * SCALE)
            shift = new_top * SCALE
            weights = [jnp.exp2(s * SCALE - shift) for s in scores]
            summed = weights[0]
            for w in weights[1:]:
                summed = summed + w
            mass = mass * fade + jnp.sum(summed, axis=0, keepdims=True)
            part = over_keys(
                jnp.concatenate([rows_of(v_ref, b) for b in blocks], axis=0),
                jnp.concatenate([w.astype(jnp.bfloat16) for w in weights], axis=0),
            )
            total[...] = total[...] * fade + part
            return new_top, mass

        groups = count // GROUP
        state = lax.fori_loop(0, groups, lambda t, c: add(t * GROUP, GROUP, c), (top, mass))
        top, mass = lax.fori_loop(groups * GROUP, count, lambda t, c: add(t, 1, c), state)
        result = total[...] / mass
        for h in range(H):
            out_ref[rows, h * DH : (h + 1) * DH] = result[:, h * BLOCK : (h + 1) * BLOCK].T


def shards(queries, keys, values, block_mask):
    all_keys = lax.all_gather(keys, ("kcol", "qrow"), axis=0, tiled=True)
    all_values = lax.all_gather(values, ("kcol", "qrow"), axis=0, tiled=True)
    vmem = pl.BlockSpec(memory_space=pltpu.VMEM)
    return pl.pallas_call(
        attend,
        out_shape=jax.ShapeDtypeStruct(queries.shape, jnp.float32),
        in_specs=[pl.BlockSpec(memory_space=pltpu.SMEM), vmem, vmem, vmem],
        out_specs=vmem,
        scratch_shapes=[
            pltpu.SMEM((block_mask.shape[1],), jnp.int32),
            pltpu.VMEM((DH, H * BLOCK), jnp.float32),
        ],
        compiler_params=pltpu.CompilerParams(vmem_limit_bytes=48 * 2**20),
    )(block_mask, queries, all_keys, all_values)


def solution(mesh):
    placed = (P(("qrow", "kcol"), None), P(("kcol", "qrow"), None), P(("kcol", "qrow"), None), P())
    return jax.shard_map(
        shards, mesh=mesh, in_specs=placed, out_specs=P(("qrow", "kcol"), None), check_vma=False
    )
```

time: 248 us -> 150 us (0.60)
  the two profiles are of different devices: /device:TPU:0 before, /device:TPU:31 now
where the time goes in v1:
time: 150 us
  waiting for transfers between devices  117 us (78%)
  Pallas kernels  14.1 us (9%)
  between operations  13.4 us (9%)
  local copies, waits for them, and re-layouts  4.89 us (3%)
    all_gather x1, waiting for transfers between devices, shards(): all_values = lax.all_gather(values, ('kcol', 'qrow'), axis=0, tiled=True)  58 us
    all_gather x1, waiting for transfers between devices, shards(): all_keys = lax.all_gather(keys, ('kcol', 'qrow'), axis=0, tiled=True)  57.7 us
    pallas_call x1, Pallas kernels, shards(): pl.pallas_call(attend, out_shape=jax.ShapeDtypeStruct(queries.shape, jnp....  14.1 us
    unnamed x8, local copies, waits for them, and re-layouts  4.89 us
  transfers between devices with their start and end apart: 2, of which 2 were waited for; matrix products, arithmetic and copies ran while one was open for 0% of the time, Pallas kernels for 0%

profile of v1, /device:TPU:31, one launch (start us, length us, event | category | flops | bytes accessed | tf_op | source)
XLA Modules:
  0.0 149.5 jit_solution(1484014347211720192)
XLA Ops:
  6.5 0.0 all-gather.3.cloned.1.call-start
  6.5 0.7 all-gather.3.cloned.1.call-update
  7.3 0.0 all-gather.5.cloned.1.call-start
  7.3 0.7 all-gather.5.cloned.1.call-update
  8.0 57.7 %all-gather.3.cloned.1.call-done.k_ref = bf16[8192,128]{1,0:T(8,128)(2,1)} async-done(((bf16[256,128]{1,0:T(8,128)(2,1)}), bf16[8192,128]{1,0:T(8,128)(2,1)}) %all-gather.3.cloned.1.call-update) | async-done | bytes 2097168 | tf_op jit(solution)/shard_map/all_gather | solution.py:87
  65.7 58.0 %all-gather.5.cloned.1.call-done.v_ref = bf16[8192,128]{1,0:T(8,128)(2,1)} async-done(((bf16[256,128]{1,0:T(8,128)(2,1)}), bf16[8192,128]{1,0:T(8,128)(2,1)}) %all-gather.5.cloned.1.call-update) | async-done | bytes 2097168 | tf_op jit(solution)/shard_map/all_gather | solution.py:88
  123.7 0.0 copy-start
  123.7 1.6 %copy-done = bf16[8192,128]{1,0:T(8,128)(2,1)S(1)} copy-done((bf16[8192,128]{1,0:T(8,128)(2,1)S(1)}, bf16[8192,128]{1,0:T(8,128)(2,1)}, u32[]{:S(2)}) %copy-start) | copy-done | bytes 2097176
  125.3 0.0 copy-start.1
  125.3 1.6 %copy-done.1 = bf16[8192,128]{1,0:T(8,128)(2,1)S(1)} copy-done((bf16[8192,128]{1,0:T(8,128)(2,1)S(1)}, bf16[8192,128]{1,0:T(8,128)(2,1)}, u32[]{:S(2)}) %copy-start.1) | copy-done | bytes 2097176
  126.9 0.0 copy-start.2
  126.9 0.9 copy-done.2
  127.8 0.0 copy-start.3
  127.8 0.8 copy-done.3
  128.6 14.1 %shard_map.46 = f32[256,512]{1,0:T(8,128)} custom-call(s32[64,64]{1,0:T(8,128)S(1)} %copy-done.3, bf16[256,512]{1,0:T(8,128)(2,1)S(1)} %copy-done.2, bf16[8192,128]{1,0:T(8,128)(2,1)S(1)} %copy-done, bf16[8192,128]{1,0:T(8,128)(2,1)S(1)} %copy-done.1), custom_call_target="tpu_custom_call" | custom-call | tf_op jit(solution)/shard_map/pallas_call | solution.py:90
Async XLA Ops:
  6.5 59.2 %all-gather.3.cloned.1.call-start = ((), (), s32[]{:S(2)}) async-start(), calls=%async_computation | async-start | bytes 2162688 | tf_op jit(solution)/shard_map/all_gather | solution.py:87
  7.3 116.4 %all-gather.5.cloned.1.call-start = ((), (), s32[]{:S(2)}) async-start(), calls=%async_computation.1 | async-start | bytes 2162688 | tf_op jit(solution)/shard_map/all_gather | solution.py:88
  123.7 1.6 %copy-start = (bf16[8192,128]{1,0:T(8,128)(2,1)S(1)}, bf16[8192,128]{1,0:T(8,128)(2,1)}, u32[]{:S(2)}) copy-start(bf16[8192,128]{1,0:T(8,128)(2,1)} %all-gather.3.cloned.1.call-done.k_ref) | copy-start | bytes 6291460
  125.3 1.6 %copy-start.1 = (bf16[8192,128]{1,0:T(8,128)(2,1)S(1)}, bf16[8192,128]{1,0:T(8,128)(2,1)}, u32[]{:S(2)}) copy-start(bf16[8192,128]{1,0:T(8,128)(2,1)} %all-gather.5.cloned.1.call-done.v_ref) | copy-start | bytes 6291460
  126.9 0.9 copy-start.2
  127.8 0.8 copy-start.3
Sparse Core Ops, SparseCore 0:
  10.2 55.4 all-gather.2
  68.6 55.0 all-gather.4

commit v2 on v1

--- a/solution.py
+++ b/solution.py
@@ -11,6 +11,7 @@
 DH = 128
 BLOCK = 128
 GROUP = 4
+MOST = 64
 NEG_FILL = -1e30
 SCALE = math.log2(math.e) / math.sqrt(DH)
 
@@ -83,9 +84,180 @@
             out_ref[rows, h * DH : (h + 1) * DH] = result[:, h * BLOCK : (h + 1) * BLOCK].T
 
 
+def spread(k_ref, v_ref, k_all, v_all, send, recv, local):
+    ring, lane = lax.axis_size("kcol"), lax.axis_size("qrow")
+    depth, width = ring // 2, lane // 2
+    q, c = lax.axis_index("qrow"), lax.axis_index("kcol")
+    level, core = c // 2, c % 2
+    high, low = q // width, q % width
+    tokens = k_ref.shape[0]
+    own, whole = (k_ref, v_ref), (k_all, v_all)
+    sibling = {"qrow": q, "kcol": level * 2 + (1 - core)}
+    over = {"qrow": (1 - high) * width + low, "kcol": c}
+    sides = [(low + i) % width for i in range(1, width)]
+    beside = [{"qrow": high * width + i, "kcol": c} for i in sides]
+    up = {"qrow": q, "kcol": c + 2}
+    down = {"qrow": q, "kcol": c - 2}
+    has_up, has_down = level < depth - 1, level > 0
+
+    def slot(at, column, parity=core):
+        return (at * 2 + parity) * lane + column
+
+    def place(kv, block):
+        return whole[kv].at[pl.ds(pl.multiple_of(block * tokens, tokens), tokens), :]
+
+    barrier = pltpu.get_barrier_semaphore()
+
+    def greet(target):
+        pl.semaphore_signal(
+            barrier, inc=1, device_id=target, device_id_type=pl.DeviceIdType.MESH
+        )
+
+    for target in [sibling, over] + beside:
+        greet(target)
+    pl.when(has_up)(lambda: greet(up))
+    pl.when(has_down)(lambda: greet(down))
+    ends = has_up.astype(jnp.int32) + has_down.astype(jnp.int32)
+    pl.semaphore_wait(barrier, 2 + len(beside) + ends)
+
+    started = []
+
+    def landed(ok, kv, block):
+        @pl.when(ok)
+        def _():
+            here = place(kv, block)
+            pltpu.make_async_copy(here, here, recv.at[kv, block]).wait()
+
+    def push(ok, kv, block, target, kind, at, source=None):
+        copy = pltpu.make_async_remote_copy(
+            src_ref=place(kv, block) if source is None else source,
+            dst_ref=place(kv, block),
+            send_sem=send.at[kind, at],
+            recv_sem=recv.at[kv, block],
+            device_id=target,
+            device_id_type=pl.DeviceIdType.MESH,
+        )
+        pl.when(ok)(copy.start)
+        started.append((ok, copy))
+
+    def column_sends(ok, at, way):
+        block = slot(at, q)
+        for kv in range(2):
+            source = own[kv] if way == 0 else None
+            if way == 0:
+                push(has_up, kv, block, up, 0 + kv, at, source)
+                push(has_down, kv, block, down, 2 + kv, at, source)
+            else:
+                landed(ok, kv, block)
+                if way > 0:
+                    push(ok & has_up, kv, block, up, 0 + kv, at)
+                else:
+                    push(ok & has_down, kv, block, down, 2 + kv, at)
+            push(ok, kv, block, over, 4 + kv, at, source)
+            for i, target in enumerate(beside):
+                push(ok, kv, block, target, 8 + 2 * i + kv, at, source)
+            push(ok, kv, block, sibling, 6 + kv, at, source)
+
+    base = 8 + 2 * len(beside)
+
+    def relays(ok, at):
+        kind = base
+        for i in sides:
+            block = slot(at, high * width + i)
+            landed(ok, 0, block)
+            push(ok, 0, block, over, kind, at)
+            push(ok, 0, block, sibling, kind + 1, at)
+            kind += 2
+        block = slot(at, (1 - high) * width + low)
+        for kv in (1, 0):
+            landed(ok, kv, block)
+            if kv == 1:
+                for target in beside:
+                    push(ok, 1, block, target, kind, at)
+                    kind += 1
+            push(ok, kv, block, sibling, kind, at)
+            kind += 1
+        for i in sides:
+            block = slot(at, high * width + i)
+            landed(ok, 1, block)
+            push(ok, 1, block, sibling, kind, at)
+            kind += 1
+
+    last = base + 4 * len(beside) + 2
+
+    def corners(ok, at):
+        kind = last
+        for i in sides:
+            block = slot(at, (1 - high) * width + i)
+            for kv in range(2):
+                landed(ok, kv, block)
+                push(ok, kv, block, sibling, kind, at)
+                kind += 1
+
+    def positions(step):
+        if step == 0:
+            return [(level >= 0, level, 0)]
+        return [
+            (level >= step, level - step, 1),
+            (level + step < depth, level + step, -1),
+        ]
+
+    copies = []
+    for step in range(depth + 2):
+        if step < depth:
+            for ok, at, way in positions(step):
+                column_sends(ok, at, way)
+        if step == 0:
+            for kv in range(2):
+                copy = pltpu.make_async_copy(own[kv], place(kv, slot(level, q)), local.at[kv])
+                copy.start()
+                copies.append(copy)
+        if 1 <= step <= depth:
+            for ok, at, _ in positions(step - 1):
+                relays(ok, at)
+        if step >= 2:
+            for ok, at, _ in positions(step - 2):
+                corners(ok, at)
+    for copy in copies:
+        copy.wait()
+    for at in range(depth):
+        for column in range(lane):
+            for kv in range(2):
+                landed(level >= 0, kv, slot(at, column, 1 - core))
+    for ok, copy in started:
+        pl.when(ok)(copy.wait_send)
+
+
+def gathered(keys, values):
+    ring, lane = lax.axis_size("kcol"), lax.axis_size("qrow")
+    devices = ring * lane
+    if ring % 2 or lane % 2 or devices > MOST:
+        both = ("kcol", "qrow")
+        return (
+            lax.all_gather(keys, both, axis=0, tiled=True),
+            lax.all_gather(values, both, axis=0, tiled=True),
+        )
+    vmem = pl.BlockSpec(memory_space=pltpu.VMEM)
+    full = jax.ShapeDtypeStruct((keys.shape[0] * devices, keys.shape[1]), keys.dtype)
+    side = lane // 2 - 1
+    return pl.pallas_call(
+        spread,
+        out_shape=(full, full),
+        in_specs=[vmem, vmem],
+        out_specs=(vmem, vmem),
+        scratch_shapes=[
+            pltpu.SemaphoreType.DMA((10 + 8 * side, ring // 2)),
+            pltpu.SemaphoreType.DMA((2, devices)),
+            pltpu.SemaphoreType.DMA((2,)),
+        ],
+        compiler_params=pltpu.CompilerParams(
+            collective_id=0, has_side_effects=True, vmem_limit_bytes=32 * 2**20
+        ),
+    )(keys, values)
+
+
 def shards(queries, keys, values, block_mask):
-    all_keys = lax.all_gather(keys, ("kcol", "qrow"), axis=0, tiled=True)
-    all_values = lax.all_gather(values, ("kcol", "qrow"), axis=0, tiled=True)
+    all_keys, all_values = gathered(keys, values)
     vmem = pl.BlockSpec(memory_space=pltpu.VMEM)
     return pl.pallas_call(
         attend,

time: 150 us -> 41.1 us (0.27)
  waiting for transfers between devices: 117 us -> 0 us
  Pallas kernels: 14.1 us -> 37.9 us
  between operations: 13.4 us -> 0.02 us
  local copies, waits for them, and re-layouts: 4.89 us -> 3.38 us
    all_gather x2 -> x0, waiting for transfers between devices: 116 us -> none  [the longest x1 58 us: shards(): all_values = lax.all_gather(values, ('kcol', 'qrow'), axis=0, tiled=True)]
    pallas_call x0 -> x1, Pallas kernels: none -> 23.5 us  [gathered(): pl.pallas_call(spread, out_shape=(full, full), in_specs=[vmem, vmem], out...]
    unnamed x8, local copies, waits for them, and re-layouts: 4.89 us -> 3.38 us
  transfers between devices with their start and end apart: 2 -> 0, of which waited for: 2 -> 0; matrix products, arithmetic and copies ran while one was open for 0% -> 0% of each run, Pallas kernels for 0% -> 0%
where the time goes in v2:
time: 41.1 us; the launch traced here: 41.3 us
  Pallas kernels  37.9 us (92%)
  local copies, waits for them, and re-layouts  3.38 us (8%)
    pallas_call x1, Pallas kernels, gathered(): pl.pallas_call(spread, out_shape=(full, full), in_specs=[vmem, vmem], out...  23.5 us
    pallas_call x1, Pallas kernels, shards(): pl.pallas_call(attend, out_shape=jax.ShapeDtypeStruct(queries.shape, jnp....  14.4 us
    unnamed x8, local copies, waits for them, and re-layouts  3.38 us

profile of v2, /device:TPU:31, one launch (start us, length us, event | category | flops | bytes accessed | tf_op | source)
XLA Modules:
  0.0 41.3 jit_solution(11612697232078493295)
XLA Ops:
  0.0 0.0 copy-start.1
  0.0 0.8 %copy-done.1 = bf16[256,128]{1,0:T(8,128)(2,1)S(1)} copy-done((bf16[256,128]{1,0:T(8,128)(2,1)S(1)}, bf16[256,128]{1,0:T(8,128)(2,1)}, u32[]{:S(2)}) %copy-start.1) | copy-done | bytes 65560
  0.8 0.0 copy-start.2
  0.8 0.8 %copy-done.2 = bf16[256,128]{1,0:T(8,128)(2,1)S(1)} copy-done((bf16[256,128]{1,0:T(8,128)(2,1)S(1)}, bf16[256,128]{1,0:T(8,128)(2,1)}, u32[]{:S(2)}) %copy-start.2) | copy-done | bytes 65560
  1.7 23.5 %shard_map.46 = (bf16[8192,128]{1,0:T(8,128)(2,1)S(1)}, bf16[8192,128]{1,0:T(8,128)(2,1)S(1)}) custom-call(bf16[256,128]{1,0:T(8,128)(2,1)S(1)} %copy-done.1, bf16[256,128]{1,0:T(8,128)(2,1)S(1)} %copy-done.2), custom_call_target="tpu_custom_call" | custom-call | tf_op jit(solution)/shard_map/pallas_call | solution.py:243
  25.2 0.0 copy-start
  25.2 0.9 %copy-done = bf16[256,512]{1,0:T(8,128)(2,1)S(1)} copy-done((bf16[256,512]{1,0:T(8,128)(2,1)S(1)}, bf16[256,512]{1,0:T(8,128)(2,1)}, u32[]{:S(2)}) %copy-start) | copy-done | bytes 262168
  26.1 0.0 copy-start.3
  26.1 0.8 %copy-done.3 = s32[64,64]{1,0:T(8,128)S(1)} copy-done((s32[64,64]{1,0:T(8,128)S(1)}, s32[64,64]{1,0:T(8,128)}, u32[]{:S(2)}) %copy-start.3) | copy-done | bytes 16408
  26.9 14.4 %shard_map.47 = f32[256,512]{1,0:T(8,128)} custom-call(s32[64,64]{1,0:T(8,128)S(1)} %copy-done.3, bf16[256,512]{1,0:T(8,128)(2,1)S(1)} %copy-done, bf16[8192,128]{1,0:T(8,128)(2,1)S(1)} %get-tuple-element.7.k_ref, bf16[8192,128]{1,0:T(8,128)(2,1)S(1)} %get-tuple-element.8.v_ref), custom_call_target="tpu_custom_call" | custom-call | tf_op jit(solution)/shard_map/pallas_call | solution.py:262
Async XLA Ops:
  0.0 0.8 %copy-start.1 = (bf16[256,128]{1,0:T(8,128)(2,1)S(1)}, bf16[256,128]{1,0:T(8,128)(2,1)}, u32[]{:S(2)}) copy-start(bf16[256,128]{1,0:T(8,128)(2,1)} %k_ref.1) | copy-start | bytes 196612
  0.8 0.8 %copy-start.2 = (bf16[256,128]{1,0:T(8,128)(2,1)S(1)}, bf16[256,128]{1,0:T(8,128)(2,1)}, u32[]{:S(2)}) copy-start(bf16[256,128]{1,0:T(8,128)(2,1)} %v_ref.1) | copy-start | bytes 196612
  25.2 1.0 %copy-start = (bf16[256,512]{1,0:T(8,128)(2,1)S(1)}, bf16[256,512]{1,0:T(8,128)(2,1)}, u32[]{:S(2)}) copy-start(bf16[256,512]{1,0:T(8,128)(2,1)} %q_ref.1) | copy-start | bytes 786436
  26.1 0.8 %copy-start.3 = (s32[64,64]{1,0:T(8,128)S(1)}, s32[64,64]{1,0:T(8,128)}, u32[]{:S(2)}) copy-start(s32[64,64]{1,0:T(8,128)} %mask_ref.1) | copy-start | bytes 49156

commit v3 on v2

--- a/solution.py
+++ b/solution.py
@@ -10,7 +10,7 @@
 H = 4
 DH = 128
 BLOCK = 128
-GROUP = 4
+GROUPS = (8, 4, 2, 1)
 MOST = 64
 NEG_FILL = -1e30
 SCALE = math.log2(math.e) / math.sqrt(DH)
@@ -22,13 +22,14 @@
     )
 
 
-def attend(mask_ref, q_ref, k_ref, v_ref, out_ref, listed, total):
+def attend(mask_ref, q_ref, k_ref, v_ref, out_ref, listed, total, held, sent):
     own_blocks = q_ref.shape[0] // BLOCK
     device = lax.axis_index("qrow") * lax.axis_size("kcol") + lax.axis_index("kcol")
 
     def rows_of(ref, block):
         return ref[pl.ds(pl.multiple_of(block * BLOCK, BLOCK), BLOCK), :]
 
+    copies = []
     for own in range(own_blocks):
         rows = pl.ds(own * BLOCK, BLOCK)
         row = device * own_blocks + own
@@ -76,12 +77,22 @@
             total[...] = total[...] * fade + part
             return new_top, mass
 
-        groups = count // GROUP
-        state = lax.fori_loop(0, groups, lambda t, c: add(t * GROUP, GROUP, c), (top, mass))
-        top, mass = lax.fori_loop(groups * GROUP, count, lambda t, c: add(t, 1, c), state)
+        state, done = (top, mass), jnp.int32(0)
+        for size in GROUPS:
+            trips = (count - done) // size
+            state = lax.fori_loop(
+                0, trips, lambda t, c: add(done + t * size, size, c), state
+            )
+            done = done + trips * size
+        mass = state[1]
         result = total[...] / mass
         for h in range(H):
-            out_ref[rows, h * DH : (h + 1) * DH] = result[:, h * BLOCK : (h + 1) * BLOCK].T
+            held[rows, h * DH : (h + 1) * DH] = result[:, h * BLOCK : (h + 1) * BLOCK].T
+        copy = pltpu.make_async_copy(held.at[rows, :], out_ref.at[rows, :], sent.at[own])
+        copy.start()
+        copies.append(copy)
+    for copy in copies:
+        copy.wait()
 
 
 def spread(k_ref, v_ref, k_all, v_all, send, recv, local):
@@ -106,6 +117,12 @@
     def place(kv, block):
         return whole[kv].at[pl.ds(pl.multiple_of(block * tokens, tokens), tokens), :]
 
+    copies = [
+        pltpu.make_async_copy(own[kv], place(kv, slot(level, q)), local.at[kv]) for kv in range(2)
+    ]
+    for copy in copies:
+        copy.start()
+
     barrier = pltpu.get_barrier_semaphore()
 
     def greet(target):
@@ -120,6 +137,8 @@
     ends = has_up.astype(jnp.int32) + has_down.astype(jnp.int32)
     pl.semaphore_wait(barrier, 2 + len(beside) + ends)
 
+    for copy in copies:
+        copy.wait()
     started = []
 
     def landed(ok, kv, block):
@@ -128,9 +147,9 @@
             here = place(kv, block)
             pltpu.make_async_copy(here, here, recv.at[kv, block]).wait()
 
-    def push(ok, kv, block, target, kind, at, source=None):
+    def push(ok, kv, block, target, kind, at):
         copy = pltpu.make_async_remote_copy(
-            src_ref=place(kv, block) if source is None else source,
+            src_ref=place(kv, block),
             dst_ref=place(kv, block),
             send_sem=send.at[kind, at],
             recv_sem=recv.at[kv, block],
@@ -143,20 +162,19 @@
     def column_sends(ok, at, way):
         block = slot(at, q)
         for kv in range(2):
-            source = own[kv] if way == 0 else None
             if way == 0:
-                push(has_up, kv, block, up, 0 + kv, at, source)
-                push(has_down, kv, block, down, 2 + kv, at, source)
+                push(has_up, kv, block, up, 0 + kv, at)
+                push(has_down, kv, block, down, 2 + kv, at)
             else:
                 landed(ok, kv, block)
                 if way > 0:
                     push(ok & has_up, kv, block, up, 0 + kv, at)
                 else:
                     push(ok & has_down, kv, block, down, 2 + kv, at)
-            push(ok, kv, block, over, 4 + kv, at, source)
+            push(ok, kv, block, over, 4 + kv, at)
             for i, target in enumerate(beside):
-                push(ok, kv, block, target, 8 + 2 * i + kv, at, source)
-            push(ok, kv, block, sibling, 6 + kv, at, source)
+                push(ok, kv, block, target, 8 + 2 * i + kv, at)
+            push(ok, kv, block, sibling, 6 + kv, at)
 
     base = 8 + 2 * len(beside)
 
@@ -202,24 +220,16 @@
             (level + step < depth, level + step, -1),
         ]
 
-    copies = []
     for step in range(depth + 2):
         if step < depth:
             for ok, at, way in positions(step):
                 column_sends(ok, at, way)
-        if step == 0:
-            for kv in range(2):
-                copy = pltpu.make_async_copy(own[kv], place(kv, slot(level, q)), local.at[kv])
-                copy.start()
-                copies.append(copy)
         if 1 <= step <= depth:
             for ok, at, _ in positions(step - 1):
                 relays(ok, at)
         if step >= 2:
             for ok, at, _ in positions(step - 2):
                 corners(ok, at)
-    for copy in copies:
-        copy.wait()
     for at in range(depth):
         for column in range(lane):
             for kv in range(2):
@@ -243,7 +253,7 @@
     return pl.pallas_call(
         spread,
         out_shape=(full, full),
-        in_specs=[vmem, vmem],
+        in_specs=[pl.BlockSpec(memory_space=pltpu.HBM)] * 2,
         out_specs=(vmem, vmem),
         scratch_shapes=[
             pltpu.SemaphoreType.DMA((10 + 8 * side, ring // 2)),
@@ -263,10 +273,12 @@
         attend,
         out_shape=jax.ShapeDtypeStruct(queries.shape, jnp.float32),
         in_specs=[pl.BlockSpec(memory_space=pltpu.SMEM), vmem, vmem, vmem],
-        out_specs=vmem,
+        out_specs=pl.BlockSpec(memory_space=pltpu.HBM),
         scratch_shapes=[
             pltpu.SMEM((block_mask.shape[1],), jnp.int32),
             pltpu.VMEM((DH, H * BLOCK), jnp.float32),
+            pltpu.VMEM(queries.shape, jnp.float32),
+            pltpu.SemaphoreType.DMA((queries.shape[0] // BLOCK,)),
         ],
         compiler_params=pltpu.CompilerParams(vmem_limit_bytes=48 * 2**20),
     )(block_mask, queries, all_keys, all_values)

time: 41.1 us -> 39.3 us (0.956); the launches traced: 41.3 us -> 39.1 us
  Pallas kernels: 37.9 us -> 35.7 us
    pallas_call x1, Pallas kernels: 14.4 us -> 12 us  [shards(): pl.pallas_call(attend, out_shape=jax.ShapeDtypeStruct(queries.shape, jnp....]
where the time goes in v3:
time: 39.3 us; the launch traced here: 39.1 us
  Pallas kernels  35.7 us (91%)
  local copies, waits for them, and re-layouts  3.38 us (9%)
    pallas_call x1, Pallas kernels, gathered(): pl.pallas_call(spread, out_shape=(full, full), in_specs=[pl.BlockSpec(mem...  23.6 us
    pallas_call x1, Pallas kernels, shards(): pl.pallas_call(attend, out_shape=jax.ShapeDtypeStruct(queries.shape, jnp....  12 us
    unnamed x8, local copies, waits for them, and re-layouts  3.38 us

profile of v3, /device:TPU:31, one launch (start us, length us, event | category | flops | bytes accessed | tf_op | source)
XLA Modules:
  0.0 39.1 jit_solution(3515557031096121859)
XLA Ops:
  0.0 0.0 copy-start.1
  0.0 0.8 %copy-done.1 = bf16[256,128]{1,0:T(8,128)(2,1)S(1)} copy-done((bf16[256,128]{1,0:T(8,128)(2,1)S(1)}, bf16[256,128]{1,0:T(8,128)(2,1)}, u32[]{:S(2)}) %copy-start.1) | copy-done | bytes 65560
  0.8 0.0 copy-start.2
  0.8 0.8 %copy-done.2 = bf16[256,128]{1,0:T(8,128)(2,1)S(1)} copy-done((bf16[256,128]{1,0:T(8,128)(2,1)S(1)}, bf16[256,128]{1,0:T(8,128)(2,1)}, u32[]{:S(2)}) %copy-start.2) | copy-done | bytes 65560
  1.7 23.6 %shard_map.46 = (bf16[8192,128]{1,0:T(8,128)(2,1)S(1)}, bf16[8192,128]{1,0:T(8,128)(2,1)S(1)}) custom-call(bf16[256,128]{1,0:T(8,128)(2,1)S(1)} %copy-done.1, bf16[256,128]{1,0:T(8,128)(2,1)S(1)} %copy-done.2), custom_call_target="tpu_custom_call" | custom-call | tf_op jit(solution)/shard_map/pallas_call | solution.py:253
  25.3 0.0 copy-start
  25.3 0.9 %copy-done = bf16[256,512]{1,0:T(8,128)(2,1)S(1)} copy-done((bf16[256,512]{1,0:T(8,128)(2,1)S(1)}, bf16[256,512]{1,0:T(8,128)(2,1)}, u32[]{:S(2)}) %copy-start) | copy-done | bytes 262168
  26.3 0.0 copy-start.3
  26.3 0.8 %copy-done.3 = s32[64,64]{1,0:T(8,128)S(1)} copy-done((s32[64,64]{1,0:T(8,128)S(1)}, s32[64,64]{1,0:T(8,128)}, u32[]{:S(2)}) %copy-start.3) | copy-done | bytes 16408
  27.0 12.0 %shard_map.47 = f32[256,512]{1,0:T(8,128)} custom-call(s32[64,64]{1,0:T(8,128)S(1)} %copy-done.3, bf16[256,512]{1,0:T(8,128)(2,1)S(1)} %copy-done, bf16[8192,128]{1,0:T(8,128)(2,1)S(1)} %get-tuple-element.7.k_ref, bf16[8192,128]{1,0:T(8,128)(2,1)S(1)} %get-tuple-element.8.v_ref), custom_call_target="tpu_custom_call" | custom-call | tf_op jit(solution)/shard_map/pallas_call | solution.py:272
Async XLA Ops:
  0.0 0.8 %copy-start.1 = (bf16[256,128]{1,0:T(8,128)(2,1)S(1)}, bf16[256,128]{1,0:T(8,128)(2,1)}, u32[]{:S(2)}) copy-start(bf16[256,128]{1,0:T(8,128)(2,1)} %k_ref.1) | copy-start | bytes 196612
  0.8 0.8 %copy-start.2 = (bf16[256,128]{1,0:T(8,128)(2,1)S(1)}, bf16[256,128]{1,0:T(8,128)(2,1)}, u32[]{:S(2)}) copy-start(bf16[256,128]{1,0:T(8,128)(2,1)} %v_ref.1) | copy-start | bytes 196612
  25.3 1.0 %copy-start = (bf16[256,512]{1,0:T(8,128)(2,1)S(1)}, bf16[256,512]{1,0:T(8,128)(2,1)}, u32[]{:S(2)}) copy-start(bf16[256,512]{1,0:T(8,128)(2,1)} %q_ref.1) | copy-start | bytes 786436
  26.3 0.8 %copy-start.3 = (s32[64,64]{1,0:T(8,128)S(1)}, s32[64,64]{1,0:T(8,128)}, u32[]{:S(2)}) copy-start(s32[64,64]{1,0:T(8,128)} %mask_ref.1) | copy-start | bytes 49156

commit v4 on v3

--- a/solution.py
+++ b/solution.py
@@ -238,6 +238,10 @@
         pl.when(ok)(copy.wait_send)
 
 
+def in_hbm(array):
+    return pltpu.with_memory_space_constraint(array, pltpu.HBM)
+
+
 def gathered(keys, values):
     ring, lane = lax.axis_size("kcol"), lax.axis_size("qrow")
     devices = ring * lane
@@ -263,7 +267,7 @@
         compiler_params=pltpu.CompilerParams(
             collective_id=0, has_side_effects=True, vmem_limit_bytes=32 * 2**20
         ),
-    )(keys, values)
+    )(in_hbm(keys), in_hbm(values))
 
 
 def shards(queries, keys, values, block_mask):
@@ -281,7 +285,7 @@
             pltpu.SemaphoreType.DMA((queries.shape[0] // BLOCK,)),
         ],
         compiler_params=pltpu.CompilerParams(vmem_limit_bytes=48 * 2**20),
-    )(block_mask, queries, all_keys, all_values)
+    )(in_hbm(block_mask), queries, all_keys, all_values)
 
 
 def solution(mesh):

time: 39.3 us -> 36.3 us (0.924)
  local copies, waits for them, and re-layouts: 3.38 us -> 0.95 us
  Pallas kernels: 35.7 us -> 35 us
    unnamed x8 -> x2, local copies, waits for them, and re-layouts: 3.38 us -> 0.95 us
    pallas_call x1, Pallas kernels: 12 us -> 11.5 us  [shards(): pl.pallas_call(attend, out_shape=jax.ShapeDtypeStruct(queries.shape, jnp....]
where the time goes in v4:
time: 36.3 us; the launch traced here: 35.9 us
  Pallas kernels  35 us (96%)
  local copies, waits for them, and re-layouts  0.95 us (3%)
    pallas_call x1, Pallas kernels, gathered(): pl.pallas_call(spread, out_shape=(full, full), in_specs=[pl.BlockSpec(mem...  23.5 us
    pallas_call x1, Pallas kernels, shards(): pl.pallas_call(attend, out_shape=jax.ShapeDtypeStruct(queries.shape, jnp....  11.5 us
    unnamed x2, local copies, waits for them, and re-layouts  0.95 us

profile of v4, /device:TPU:31, one launch (start us, length us, event | category | flops | bytes accessed | tf_op | source)
XLA Modules:
  0.0 35.9 jit_solution(17687384041735777754)
XLA Ops:
  0.0 23.5 %shard_map.46 = (bf16[8192,128]{1,0:T(8,128)(2,1)S(1)}, bf16[8192,128]{1,0:T(8,128)(2,1)S(1)}) custom-call(bf16[256,128]{1,0:T(8,128)(2,1)} %k_ref.1, bf16[256,128]{1,0:T(8,128)(2,1)} %v_ref.1), custom_call_target="tpu_custom_call" | custom-call | tf_op jit(solution)/shard_map/pallas_call | solution.py:257
  23.5 0.0 copy-start
  23.5 0.9 %copy-done = bf16[256,512]{1,0:T(8,128)(2,1)S(1)} copy-done((bf16[256,512]{1,0:T(8,128)(2,1)S(1)}, bf16[256,512]{1,0:T(8,128)(2,1)}, u32[]{:S(2)}) %copy-start) | copy-done | bytes 262168
  24.4 11.5 %shard_map.47 = f32[256,512]{1,0:T(8,128)} custom-call(s32[64,64]{1,0:T(8,128)} %mask_ref.1, bf16[256,512]{1,0:T(8,128)(2,1)S(1)} %copy-done, bf16[8192,128]{1,0:T(8,128)(2,1)S(1)} %get-tuple-element.7.k_ref, bf16[8192,128]{1,0:T(8,128)(2,1)S(1)} %get-tuple-element.8.v_ref), custom_call_target="tpu_custom_call" | custom-call | tf_op jit(solution)/shard_map/pallas_call | solution.py:276
Async XLA Ops:
  23.5 1.0 %copy-start = (bf16[256,512]{1,0:T(8,128)(2,1)S(1)}, bf16[256,512]{1,0:T(8,128)(2,1)}, u32[]{:S(2)}) copy-start(bf16[256,512]{1,0:T(8,128)(2,1)} %q_ref.1) | copy-start | bytes 786436
